TPU v7x, 32 devices: a whole 2x2x4 slice. The times are simulated.
32 devices in a mesh: rep: 1, fsdp: 32 (over z, y, x, core).
Axes of the slice: x: 2, y: 2, z: 4, core: 2. Of those that a mesh axis runs over, the one named last changes fastest.
Arguments:
- accumulated: bfloat16 [1, 2048, 14336], P('rep', 'fsdp'), may hold values from -6 to 6
- q_start: bfloat16 [32, 14336], P(None, 'fsdp'), may hold values from -6 to 6
Outputs:
- residual_buffer: bfloat16 [1, 2048, 14336], P('rep', 'fsdp')
- basis_f32: float32 [2048, 32], P('fsdp')
- q_factor: float32 [32, 14336], P(None, 'fsdp')
All inputs are finite; a program needn't handle non-finite values.
Results may differ from a plain program's by a relative error of at most 0.0039.
Values may be sent and summed in bfloat16 or wider, within the bound.
No kernel may reach another device: no remote copies, remote signals or barrier semaphores. Data moves between devices by JAX's collectives and lax.ppermute only.
A program may use at most 64 MiB of HBM per device.

v0:
```python
import jax
import jax.numpy as jnp
from jax import lax
from jax.sharding import PartitionSpec as P

ITERS = 2


def orthonormal(p_sum):
    partial_gram = jnp.dot(p_sum.T, p_sum, precision=lax.Precision.HIGHEST)
    gram_matrix = lax.psum(partial_gram, "fsdp")
    factor = jnp.linalg.cholesky(gram_matrix)
    return lax.linalg.triangular_solve(factor, p_sum, left_side=False, lower=True, transpose_a=True)


def on_device(accumulated, q_start):
    own_rows = accumulated[0]
    replicas = lax.axis_size("rep")
    shard_cols = q_start.shape[1]
    owner_offset = lax.axis_index("fsdp") * shard_cols
    right_factor = q_start
    for iteration in range(ITERS):
        if iteration == 0:
            term = lax.dot_general(
                own_rows,
                lax.all_gather(q_start, "fsdp", axis=1, tiled=True),
                (((1,), (1,)), ((), ())),
                preferred_element_type=jnp.float32,
            )
            p_local = term
        else:
            p_local = lax.dot_general(
                own_rows, right_factor, (((1,), (1,)), ((), ())), preferred_element_type=jnp.float32
            )
        p_sum = lax.psum(p_local, "rep")
        basis_f32 = orthonormal(p_sum)
        basis_bf16 = basis_f32.astype(jnp.bfloat16)
        q_term = lax.dot_general(
            basis_bf16, own_rows, (((0,), (0,)), ((), ())), preferred_element_type=jnp.float32
        )
        q_whole = lax.psum(q_term, ("rep", "fsdp")) / replicas
        q_owned = lax.dynamic_slice_in_dim(q_whole, owner_offset, shard_cols, 1)
        right_factor = q_whole.astype(jnp.bfloat16)
    approx = lax.dot_general(
        basis_bf16, right_factor, (((1,), (0,)), ((), ())), preferred_element_type=jnp.float32
    )
    residual_buffer = (own_rows.astype(jnp.float32) - approx).astype(jnp.bfloat16)[None]
    return (residual_buffer, basis_f32, q_owned)


def solution(mesh):
    in_specs = (P("rep", "fsdp", None), P(None, "fsdp"))
    out_specs = (P("rep", "fsdp", None), P("fsdp", None), P(None, "fsdp"))
    return jax.shard_map(
        on_device, mesh=mesh, in_specs=in_specs, out_specs=out_specs, check_vma=False
    )
```

profile of v0, /device:TPU:0, one launch (start us, length us, event | category | flops | bytes accessed | tf_op | source)
XLA Modules:
  0.0 356.6 jit_solution(10952083144412553600)
XLA Ops:
  7.2 0.0 all-reduce.3.cloned.1.call-start
  7.2 46.5 %all-gather = bf16[32,448,32]{1,2,0:T(8,128)(2,1)S(1)} all-gather(bf16[1,448,32]{1,2,0:T(8,128)(2,1)} %bitcast.52), channel_id=1, replica_groups=mesh['rep'=1,'fsdp'=32] {'fsdp'}, dimensions={0}, use_global_device_ids=true | all-gather | bytes 946176 | tf_op jit(solution)/shard_map/all_gather | solution.py:26
  53.7 0.6 copy.14
  54.2 2.1 reshape.20
  56.4 0.0 copy-done
  56.4 1.8 fusion.8
  58.1 0.2 fusion.24
  58.3 36.9 %psum.26 = f32[32,32]{0,1:T(8,128)S(1)} all-reduce(f32[32,32]{0,1:T(8,128)S(1)} %fusion.24), channel_id=1, replica_groups=mesh['rep'=1,'fsdp'=32] {'fsdp'}, use_global_device_ids=true, to_apply=%region_0.0 | all-reduce | flops 1024 | bytes 8192 | tf_op jit(solution)/shard_map/psum | solution.py:11
  95.2 0.1 copy.16
  95.3 2.9 cholesky.44
  98.3 0.6 compare_reduce_fusion.1
  98.9 0.7 fusion.13
  99.6 2.4 custom-call.6
  102.0 0.2 fusion.10
  102.3 1.6 fusion.6
  103.9 59.3 %all-reduce.4 = bf16[32,14336]{1,0:T(8,128)(2,1)S(1)} all-reduce(f32[32,14336]{1,0:T(8,128)} %fusion.6), channel_id=1, replica_groups=mesh['rep'=1,'fsdp'=32] {'rep','fsdp'}, use_global_device_ids=true, to_apply=%region_3.6 | all-reduce | flops 458752 | bytes 2752512 | tf_op jit(solution)/shard_map/psum | solution.py:41
  163.2 0.6 fusion.4
  163.8 0.2 fusion.25
  164.0 37.5 %psum.36 = f32[32,32]{0,1:T(8,128)S(1)} all-reduce(f32[32,32]{0,1:T(8,128)S(1)} %fusion.25), channel_id=1, replica_groups=mesh['rep'=1,'fsdp'=32] {'fsdp'}, use_global_device_ids=true, to_apply=%region_4.7 | all-reduce | flops 1024 | bytes 8192 | tf_op jit(solution)/shard_map/psum | solution.py:11
  201.4 0.1 copy.18
  201.5 2.9 cholesky.55
  204.5 0.6 compare_reduce_fusion
  205.1 0.7 fusion.14
  205.8 2.4 custom-call.7
  208.2 0.2 convolution_bitcast_fusion
  208.5 0.0 copy-start.1
  208.5 1.6 fusion.2
  210.1 0.0 all-reduce.3.cloned.1.call-update
  210.1 134.6 %all-reduce.3.cloned.1.call-done = f32[32,14336]{1,0:T(8,128)} async-done(((f32[32,14336]{1,0:T(8,128)}), f32[32,14336]{1,0:T(8,128)}) %all-reduce.3.cloned.1.call-update) | async-done | bytes 1835024 | tf_op jit(solution)/shard_map/psum | solution.py:41
  344.7 0.0 copy-done.1
  344.7 3.4 fusion.1
  348.1 1.6 constant_dynamic-slice_fusion
  (5 shorter events, 0.1 us)
Async XLA Ops:
  7.2 337.6 %all-reduce.3.cloned.1.call-start = ((), (), s32[]{:S(2)}) async-start(), calls=%async_computation | async-start | bytes 3670016 | tf_op jit(solution)/shard_map/psum | solution.py:41
  53.7 2.7 copy-start
  208.5 136.3 %copy-start.1 = (f32[64,32]{0,1:T(8,128)}, f32[64,32]{0,1:T(8,128)S(1)}, u32[]{:S(2)}) copy-start(f32[64,32]{0,1:T(8,128)S(1)} %convolution_bitcast_fusion) | copy-start | bytes 24580
Sparse Core Ops, SparseCore 0:
  210.2 134.4 all-reduce.2
where the time goes:
time: 357 us
  blocking collectives  180 us (50%)
  waiting for transfers between devices  135 us (38%)
  between operations  14.1 us (4%)
  other arithmetic  13.4 us (4%)
  matrix products  9.79 us (3%)
  local copies, waits for them, and re-layouts  4.44 us (1%)
    psum x1, waiting for transfers between devices, on_device(): q_whole = lax.psum(q_term, ('rep', 'fsdp')) / replicas  135 us
    psum x2, blocking collectives, orthonormal(): gram_matrix = lax.psum(partial_gram, 'fsdp')  74.4 us
    psum x1, blocking collectives, on_device(): q_whole = lax.psum(q_term, ('rep', 'fsdp')) / replicas  59.3 us
    all_gather x1, blocking collectives, on_device(): lax.all_gather(q_start, 'fsdp', axis=1, tiled=True)  46.5 us
    another operation x6, other arithmetic, orthonormal(): factor = jnp.linalg.cholesky(gram_matrix)  7.19 us
  transfers between devices with their start and end apart: 1, of which 1 were waited for; matrix products, arithmetic and copies ran while one was open for 0% of the time, Pallas kernels for 0%

commit v1 on v0

--- a/solution.py
+++ b/solution.py
@@ -38,7 +38,7 @@
         q_term = lax.dot_general(
             basis_bf16, own_rows, (((0,), (0,)), ((), ())), preferred_element_type=jnp.float32
         )
-        q_whole = lax.psum(q_term, ("rep", "fsdp")) / replicas
+        q_whole = jnp.sum(lax.all_gather(q_term, ("rep", "fsdp")), axis=0) / replicas
         q_owned = lax.dynamic_slice_in_dim(q_whole, owner_offset, shard_cols, 1)
         right_factor = q_whole.astype(jnp.bfloat16)
     approx = lax.dot_general(

time: 357 us -> 834 us (2.34)
  waiting for transfers between devices: 135 us -> 632 us
  blocking collectives: 180 us -> 122 us
  other arithmetic: 13.4 us -> 51.5 us
    all_gather x0 -> x2, waiting for transfers between devices: none -> 632 us  [on_device(): lax.all_gather(q_term, ('rep', 'fsdp'))]
    psum x1 -> x0, waiting for transfers between devices: 135 us -> none  [on_device(): q_whole = lax.psum(q_term, ('rep', 'fsdp')) / replicas]
    psum x1 -> x0, blocking collectives: 59.3 us -> none  [on_device(): q_whole = lax.psum(q_term, ('rep', 'fsdp')) / replicas]
    reduce_sum x0 -> x2, other arithmetic: none -> 38.1 us  [on_device(): jnp.sum(lax.all_gather(q_term, ('rep', 'fsdp')), axis=0) / replicas]
  transfers between devices with their start and end apart: 1 -> 2, of which waited for: 1 -> 2; matrix products, arithmetic and copies ran while one was open for 0% -> 0% of each run, Pallas kernels for 0% -> 0%
where the time goes in v1:
time: 834 us; the launch traced here: 833 us
  waiting for transfers between devices  632 us (76%)
  blocking collectives  122 us (15%)
  other arithmetic  51.5 us (6%)
  between operations  14.1 us (2%)
  matrix products  9.79 us (1%)
    all_gather x2, waiting for transfers between devices, on_device(): lax.all_gather(q_term, ('rep', 'fsdp'))  632 us
    psum x2, blocking collectives, orthonormal(): gram_matrix = lax.psum(partial_gram, 'fsdp')  75.4 us
    all_gather x1, blocking collectives, on_device(): lax.all_gather(q_start, 'fsdp', axis=1, tiled=True)  46.5 us
    reduce_sum x2, other arithmetic, on_device(): jnp.sum(lax.all_gather(q_term, ('rep', 'fsdp')), axis=0) / replicas  38.1 us
  transfers between devices with their start and end apart: 2, of which 2 were waited for; matrix products, arithmetic and copies ran while one was open for 0% of the time, Pallas kernels for 0%

profile of v1, /device:TPU:0, one launch (start us, length us, event | category | flops | bytes accessed | tf_op | source)
XLA Modules:
  0.0 833.4 jit_solution(1532268846572069883)
XLA Ops:
  7.2 0.0 all-gather.6.cloned.1.call-start
  7.2 46.5 %all-gather.2 = bf16[32,448,32]{1,2,0:T(8,128)(2,1)S(1)} all-gather(bf16[1,448,32]{1,2,0:T(8,128)(2,1)} %bitcast.56), channel_id=1, replica_groups=mesh['rep'=1,'fsdp'=32] {'fsdp'}, dimensions={0}, use_global_device_ids=true | all-gather | bytes 946176 | tf_op jit(solution)/shard_map/all_gather | solution.py:26
  53.7 0.6 copy.14
  54.2 2.1 reshape.22
  56.4 1.8 fusion.8
  58.1 0.2 fusion.24
  58.3 36.9 %psum.14 = f32[32,32]{0,1:T(8,128)S(1)} all-reduce(f32[32,32]{0,1:T(8,128)S(1)} %fusion.24), channel_id=1, replica_groups=mesh['rep'=1,'fsdp'=32] {'fsdp'}, use_global_device_ids=true, to_apply=%region_0.0 | all-reduce | flops 1024 | bytes 8192 | tf_op jit(solution)/shard_map/psum | solution.py:11
  95.2 0.1 copy.16
  95.3 2.9 cholesky.44
  98.3 0.6 compare_reduce_fusion.1
  98.9 0.7 fusion.13
  99.6 2.4 custom-call.6
  102.0 0.2 fusion.10
  102.2 1.6 fusion.6
  103.9 0.0 all-gather.6.cloned.1.call-update
  103.9 0.0 all-gather.8.cloned.1.call-start
  103.9 315.6 %all-gather.6.cloned.1.call-done = f32[1024,14336]{1,0:T(8,128)} async-done(((f32[32,14336]{1,0:T(8,128)}), f32[1024,14336]{1,0:T(8,128)}) %all-gather.6.cloned.1.call-update) | async-done | bytes 58720272 | tf_op jit(solution)/shard_map/all_gather | solution.py:41
  419.6 18.5 %reduce_sum.18 = bf16[32,14336]{1,0:T(8,128)(2,1)S(1)} reduce(f32[32,32,14336]{2,1,0:T(8,128)} %bitcast.55, f32[]{:T(128)} %constant.37.clone.1), dimensions={0}, to_apply=%region_3.6 | reduce | flops 14221312 | bytes 59637764 | tf_op jit(solution)/shard_map/reduce_sum | solution.py:41
  438.1 0.6 fusion.4
  438.7 0.2 fusion.25
  438.8 38.4 %psum.15 = f32[32,32]{0,1:T(8,128)S(1)} all-reduce(f32[32,32]{0,1:T(8,128)S(1)} %fusion.25), channel_id=1, replica_groups=mesh['rep'=1,'fsdp'=32] {'fsdp'}, use_global_device_ids=true, to_apply=%region_4.7 | all-reduce | flops 1024 | bytes 8192 | tf_op jit(solution)/shard_map/psum | solution.py:11
  477.3 0.1 copy.18
  477.4 2.9 cholesky.55
  480.3 0.6 compare_reduce_fusion
  481.0 0.7 fusion.14
  481.6 2.4 custom-call.7
  484.1 0.2 convolution_bitcast_fusion
  484.3 1.6 fusion.2
  486.0 316.0 %all-gather.8.cloned.1.call-done = f32[1024,14336]{1,0:T(8,128)} async-done(((f32[32,14336]{1,0:T(8,128)}), f32[1024,14336]{1,0:T(8,128)}) %all-gather.8.cloned.1.call-update) | async-done | bytes 58720272 | tf_op jit(solution)/shard_map/all_gather | solution.py:41
  801.9 19.6 %reduce_sum.19 = f32[32,14336]{1,0:T(8,128)} reduce(f32[32,32,14336]{2,1,0:T(8,128)} %bitcast.54, f32[]{:T(128)} %constant.37.clone.1), dimensions={0}, to_apply=%region_5.8 | reduce | flops 14221312 | bytes 60555268 | tf_op jit(solution)/shard_map/reduce_sum | solution.py:41
  821.6 3.4 fusion.1
  825.0 1.6 constant_dynamic-slice_fusion
  (9 shorter events, 0.1 us)
Async XLA Ops:
  7.2 412.4 %all-gather.6.cloned.1.call-start = ((), (), s32[]{:S(2)}) async-start(), calls=%async_computation | async-start | bytes 60555264 | tf_op jit(solution)/shard_map/all_gather | solution.py:41
  53.7 2.7 copy-start
  103.9 698.0 %all-gather.8.cloned.1.call-start = ((), (), s32[]{:S(2)}) async-start(), calls=%async_computation.1 | async-start | bytes 60555264 | tf_op jit(solution)/shard_map/all_gather | solution.py:41
  484.3 337.3 %copy-start.1 = (f32[64,32]{0,1:T(8,128)}, f32[64,32]{0,1:T(8,128)S(1)}, u32[]{:S(2)}) copy-start(f32[64,32]{0,1:T(8,128)S(1)} %convolution_bitcast_fusion) | copy-start | bytes 24580
Sparse Core Ops, SparseCore 0:
  104.0 315.5 all-gather.5
  486.1 315.8 all-gather.7
